TPU v7x, 32 devices: a whole 2x2x4 slice. The times are simulated.
32 devices in a mesh: dom: 4 (over z), grp: 8 (over y, x, core).
Axes of the slice: x: 2, y: 2, z: 4, core: 2. Of those that a mesh axis runs over, the one named last changes fastest.
Arguments:
- master_rows: bfloat16 [8, 512, 512], P('grp', 'dom'), may hold values from -6 to 6
- cotangent: bfloat16 [8, 512, 512], P('grp', 'dom'), may hold values from -6 to 6
- relation_weight: bfloat16 [4, 512, 512], replicated, may hold values from -0.125 to 0.125
- self_weight: bfloat16 [512, 512], replicated, may hold values from -0.25 to 0.25
- edge_source: int32 [8, 8192], P('grp', 'dom'), may hold values from 0 to 191
- edge_target: int32 [8, 8192], P('grp', 'dom'), may hold values from 0 to 191
- edge_relation: int32 [8, 8192], P('grp', 'dom'), may hold values from 0 to 3
- send_rows: int32 [8, 256], P('grp', 'dom'), may hold values from 0 to 127
- send_counts: int32 [8, 16], P('grp', 'dom'), may hold values from 4 to 16, as said below
Outputs:
- activation: bfloat16 [8, 512, 512], P('grp', 'dom')
- input_grad: bfloat16 [8, 512, 512], P('grp', 'dom')
- weight_grads: float32 [5, 512, 512], P(None, 'grp')
Inputs may be any that keep to these rules, and one draw needn't show every extreme that they name: `send_counts`: on every device the count for some peer is exactly 16.
All inputs are finite; a program needn't handle non-finite values.
Results may differ from a plain program's by a relative error of at most 0.0061.
Values may be sent and summed in bfloat16 or wider, within the bound.
No kernel may reach another device: no remote copies, remote signals or barrier semaphores. Data moves between devices by JAX's collectives and lax.ppermute only.
A program may use at most 64 MiB of HBM per device.

v0:
```python
import jax
import jax.numpy as jnp
from jax import lax
from jax.sharding import PartitionSpec as P


def pull_rows(table, send_rows, valid):
    domains = lax.axis_size("dom")
    width = table.shape[1]
    picked = table[send_rows]
    picked = jnp.where(valid[:, None], picked, jnp.zeros_like(picked))
    moved = lax.all_to_all(
        picked.reshape(domains, -1, width), "dom", split_axis=0, concat_axis=0, tiled=True
    )
    return jnp.concatenate([table, moved.reshape(-1, width)], axis=0)


def push_rows(mirror_part, placement, own):
    domains = lax.axis_size("dom")
    width = own.shape[1]
    moved = lax.all_to_all(
        mirror_part.reshape(domains, -1, width), "dom", split_axis=0, concat_axis=0, tiled=True
    )
    return own + jnp.dot(placement, moved.reshape(-1, width), preferred_element_type=jnp.float32)


def edge_counts(sources, targets, relation, relations, local_rows):
    flat_index = (relation * local_rows + targets) * local_rows + sources
    ones = jnp.ones(sources.shape, jnp.float32)
    counted = jax.ops.segment_sum(
        ones, flat_index, num_segments=relations * local_rows * local_rows
    )
    return counted.reshape(relations, local_rows, local_rows).astype(jnp.bfloat16)


def per_device(
    master_rows,
    cotangent,
    relation_weight,
    self_weight,
    edge_source,
    edge_target,
    edge_relation,
    send_rows,
    send_counts,
):
    masters = master_rows[0]
    cotan = cotangent[0]
    sources = edge_source[0]
    targets = edge_target[0]
    relation = edge_relation[0]
    slots = send_rows[0]
    counts = send_counts[0]
    domains = lax.axis_size("dom")
    relations = relation_weight.shape[0]
    master_count = masters.shape[0]
    capacity = slots.shape[0] // domains
    valid = (jnp.arange(capacity)[None, :] < counts[:, None]).reshape(-1)
    placement = ((slots[None, :] == jnp.arange(master_count)[:, None]) & valid[None, :]).astype(
        jnp.bfloat16
    )
    table = pull_rows(masters, slots, valid)
    local_rows = table.shape[0]
    adjacency = edge_counts(sources, targets, relation, relations, local_rows)
    aggregated = jnp.einsum(
        "rij,jd->rid", adjacency, table, preferred_element_type=jnp.float32
    ).astype(jnp.bfloat16)
    partial_value = jnp.einsum(
        "rnd,rde->ne", aggregated, relation_weight, preferred_element_type=jnp.float32
    )
    own = partial_value[:master_count] + jnp.dot(
        masters, self_weight, preferred_element_type=jnp.float32
    )
    z_value = push_rows(partial_value[master_count:].astype(jnp.bfloat16), placement, own)
    activation = jax.nn.silu(z_value).astype(jnp.bfloat16)
    sigmoid_z = jax.nn.sigmoid(z_value)
    grad_z = (cotan.astype(jnp.float32) * sigmoid_z * (1.0 + z_value * (1.0 - sigmoid_z))).astype(
        jnp.bfloat16
    )
    grad_table = pull_rows(grad_z, slots, valid)
    relation_grad = jnp.einsum(
        "rnd,ne->rde", aggregated, grad_table, preferred_element_type=jnp.float32
    )
    self_grad = jnp.dot(masters.T, grad_z, preferred_element_type=jnp.float32)
    local_grads = jnp.concatenate([relation_grad, self_grad[None]], axis=0)
    group_part = lax.psum_scatter(local_grads, "grp", scatter_dimension=1, tiled=True)
    weight_grads = lax.psum(group_part, "dom")
    back = jnp.einsum(
        "rij,id->rjd", adjacency, grad_table, preferred_element_type=jnp.float32
    ).astype(jnp.bfloat16)
    back_partial = jnp.einsum(
        "rne,rde->nd", back, relation_weight, preferred_element_type=jnp.float32
    )
    back_own = back_partial[:master_count] + jnp.dot(
        grad_z, self_weight.T, preferred_element_type=jnp.float32
    )
    input_grad = push_rows(back_partial[master_count:].astype(jnp.bfloat16), placement, back_own)
    return (activation[None], input_grad.astype(jnp.bfloat16)[None], weight_grads)


def solution(mesh):
    return jax.shard_map(
        per_device,
        mesh=mesh,
        in_specs=(
            P("grp", "dom", None),
            P("grp", "dom", None),
            P(),
            P(),
            P("grp", "dom"),
            P("grp", "dom"),
            P("grp", "dom"),
            P("grp", "dom"),
            P("grp", "dom"),
        ),
        out_specs=(P("grp", "dom", None), P("grp", "dom", None), P(None, "grp", None)),
        check_vma=False,
    )
```

profile of v0, /device:TPU:0, one launch (start us, length us, event | category | flops | bytes accessed | tf_op | source)
XLA Modules:
  0.0 171.5 jit_solution(12031938624284277153)
XLA Ops:
  7.2 0.9 iota_compare_fusion.1
  8.8 1.6 gather_fusion
  11.1 6.3 %all-to-all-start = ((bf16[4,16,512]{2,1,0:T(8,128)(2,1)}), bf16[4,16,512]{2,1,0:T(8,128)(2,1)}, u32[]{:S(2)}, u32[]{:S(2)}) async-start(bf16[4,16,512]{2,1,0:T(8,128)(2,1)} %broadcast_select_fusion.1), calls=%async_computation | async-start | bytes 131072 | tf_op jit(solution)/shard_map/all_to_all | solution.py:12
  17.4 0.7 multiply_add_fusion
  18.2 11.4 %scatter_custom_fusion = f32[147456]{0:T(1024)S(1)} fusion(s32[2048]{0:T(1024)S(1)} %bitcast.64, f32[2048]{0:T(1024)S(1)} %broadcast.65, f32[]{:T(128)} %constant.6.clone.1), kind=kCustom, calls=%fused_computation.16 | custom fusion | flops 2048 | bytes 589828 | tf_op jit(solution)/shard_map/scatter-add | solution.py:30
  29.9 1.2 convolution_convert_fusion.1
  31.8 0.7 copy-done.3
  33.1 5.1 %all-to-all-start.1 = ((bf16[4,16,512]{2,1,0:T(8,128)(2,1)}), bf16[4,16,512]{2,1,0:T(8,128)(2,1)S(1)}, u32[]{:S(2)}, u32[]{:S(2)}) async-start(bf16[4,16,512]{2,1,0:T(8,128)(2,1)} %bitcast.10), calls=%async_computation.1 | async-start | bytes 131072 | tf_op jit(solution)/shard_map/all_to_all | solution.py:21
  38.3 5.7 %all-to-all-done.1 = bf16[4,16,512]{2,1,0:T(8,128)(2,1)S(1)} async-done(((bf16[4,16,512]{2,1,0:T(8,128)(2,1)}), bf16[4,16,512]{2,1,0:T(8,128)(2,1)S(1)}, u32[]{:S(2)}, u32[]{:S(2)}) %all-to-all-start.1) | async-done | bytes 65568 | tf_op jit(solution)/shard_map/all_to_all | solution.py:21
  44.1 2.2 %fusion.9 = (bf16[128,512]{1,0:T(8,128)(2,1)S(1)}, bf16[1,128,512]{2,1,0:T(8,128)(2,1)}) fusion(bf16[1,128,512]{2,1,0:T(8,128)(2,1)} %param.10, f32[128,512]{1,0:T(8,128)S(1)} %fusion.17, bf16[512,512]{1,0:T(8,128)(2,1)} %param.12, bf16[1,128,512]{2,1,0:T(8,128)(2,1)S(1)} %copy-done.1, f32[192,512]{1,0:T(8,128)} %copy-done.3), kind=kOutput, calls=%fused_computation.20 | convolution fusion | flops 68026368 | bytes 1572864 | tf_op jit(solution)/shard_map/dot_general | solution.py:71
  46.3 1.3 gather_fusion.1
  47.6 1.5 broadcast_select_fusion
  49.2 3.9 %all-to-all-start.2 = ((bf16[4,16,512]{2,1,0:T(8,128)(2,1)}), bf16[4,16,512]{2,1,0:T(8,128)(2,1)}, u32[]{:S(2)}, u32[]{:S(2)}) async-start(bf16[4,16,512]{2,1,0:T(8,128)(2,1)} %broadcast_select_fusion), calls=%async_computation.2 | async-start | bytes 131072 | tf_op jit(solution)/shard_map/all_to_all | solution.py:12
  53.1 1.3 convolution_bitcast_fusion
  54.5 4.4 %all-to-all-done.2 = bf16[4,16,512]{2,1,0:T(8,128)(2,1)} async-done(((bf16[4,16,512]{2,1,0:T(8,128)(2,1)}), bf16[4,16,512]{2,1,0:T(8,128)(2,1)}, u32[]{:S(2)}, u32[]{:S(2)}) %all-to-all-start.2) | async-done | bytes 65568 | tf_op jit(solution)/shard_map/all_to_all | solution.py:12
  58.9 1.7 fusion.13
  60.6 2.9 %pad_maximum_fusion = f32[5,512,512]{2,1,0:T(8,128)} fusion(f32[1,512,512]{2,1,0:T(8,128)S(1)} %copy-done.2, f32[4,512,512]{2,1,0:T(8,128)S(1)} %fusion.13), kind=kLoop, calls=%fused_computation.3 | loop fusion | flops 1310720 | bytes 10485760 | tf_op jit(solution)/shard_map/concatenate | solution.py:85
  63.5 55.1 %reduce-scatter.2.cloned.1.call-done = f32[5,64,512]{2,1,0:T(8,128)} async-done(((f32[5,512,512]{2,1,0:T(8,128)}), f32[5,64,512]{2,1,0:T(8,128)}) %reduce-scatter.2.cloned.1.call-update) | async-done | bytes 655376 | tf_op jit(solution)/shard_map/reduce_scatter | solution.py:86
  118.7 2.7 %fusion.1 = f32[192,512]{1,0:T(8,128)} fusion(bf16[4,512,512]{2,1,0:T(8,128)(2,1)S(1)} %copy-done, bf16[4,192,192]{2,1,0:T(8,128)(2,1)S(1)} %convert_element_type.31, bf16[64,512]{1,0:T(8,128)(2,1)} %bitcast.15, bf16[128,512]{1,0:T(8,128)(2,1)S(1)} %get-tuple-element.3), kind=kOutput, calls=%fused_computation.8 | convolution fusion | flops 554434560 | bytes 2981888 | tf_op jit(solution)/shard_map/rne,rde->nd/dot_general | solution.py:91
  121.4 0.9 slice.30
  122.3 11.1 %all_to_all.20 = bf16[4,16,512]{2,1,0:T(8,128)(2,1)S(1)} all-to-all(bf16[4,16,512]{2,1,0:T(8,128)(2,1)S(1)} %bitcast.61), channel_id=1, replica_groups=mesh['dom'=4,'grp'=8] {'dom'}, dimensions={0} | all-to-all | bytes 131072 | tf_op jit(solution)/shard_map/all_to_all | solution.py:21
  133.6 1.9 %fusion.5 = bf16[1,128,512]{2,1,0:T(8,128)(2,1)} fusion(f32[128,512]{1,0:T(8,128)S(1)} %fusion.15, bf16[128,512]{1,0:T(8,128)(2,1)S(1)} %get-tuple-element.3, bf16[512,512]{1,0:T(8,128)(2,1)S(1)} %copy-done.4, f32[192,512]{1,0:T(8,128)} %fusion.1), kind=kOutput, calls=%fused_computation.15 | convolution fusion | flops 67305472 | bytes 1310720 | tf_op jit(solution)/shard_map/dot_general | solution.py:94
  135.5 27.2 %all-reduce.2.cloned.1.call-done = f32[5,64,512]{2,1,0:T(8,128)} async-done(((f32[5,64,512]{2,1,0:T(8,128)}), f32[5,64,512]{2,1,0:T(8,128)}) %all-reduce.2.cloned.1.call-update) | async-done | bytes 655376 | tf_op jit(solution)/shard_map/psum | solution.py:87
  162.7 2.0 %copy.15 = f32[5,64,512]{2,1,0:T(8,128)} copy(f32[5,64,512]{2,1,0:T(8,128)} %all-reduce.2.cloned.1.call-done) | data formatting | bytes 1310720
  (27 shorter events, 3.4 us)
Async XLA Ops:
  7.2 24.0 %copy-start = (bf16[4,512,512]{2,1,0:T(8,128)(2,1)S(1)}, bf16[4,512,512]{2,1,0:T(8,128)(2,1)}, u32[]{:S(2)}) copy-start(bf16[4,512,512]{2,1,0:T(8,128)(2,1)} %param.11) | copy-start | bytes 6291460
  7.2 22.8 %copy-start.1 = (bf16[1,128,512]{2,1,0:T(8,128)(2,1)S(1)}, bf16[1,128,512]{2,1,0:T(8,128)(2,1)}, u32[]{:S(2)}) copy-start(bf16[1,128,512]{2,1,0:T(8,128)(2,1)} %param.9) | copy-start | bytes 393220
  11.1 18.8 %all-to-all-start = ((bf16[4,16,512]{2,1,0:T(8,128)(2,1)}), bf16[4,16,512]{2,1,0:T(8,128)(2,1)}, u32[]{:S(2)}, u32[]{:S(2)}) async-start(bf16[4,16,512]{2,1,0:T(8,128)(2,1)} %broadcast_select_fusion.1), calls=%async_computation | async-start | bytes 131072 | tf_op jit(solution)/shard_map/all_to_all | solution.py:12
  31.2 12.8 %copy-start.5 = (s32[1,64]{1,0:T(1,128)S(1)}, s32[1,64]{1,0:T(1,128)}, u32[]{:S(2)}) copy-start(s32[1,64]{1,0:T(1,128)} %param.16) | copy-start | bytes 772
  31.7 0.7 copy-start.3
  33.1 10.8 %all-to-all-start.1 = ((bf16[4,16,512]{2,1,0:T(8,128)(2,1)}), bf16[4,16,512]{2,1,0:T(8,128)(2,1)S(1)}, u32[]{:S(2)}, u32[]{:S(2)}) async-start(bf16[4,16,512]{2,1,0:T(8,128)(2,1)} %bitcast.10), calls=%async_computation.1 | async-start | bytes 131072 | tf_op jit(solution)/shard_map/all_to_all | solution.py:21
  49.2 9.7 %all-to-all-start.2 = ((bf16[4,16,512]{2,1,0:T(8,128)(2,1)}), bf16[4,16,512]{2,1,0:T(8,128)(2,1)}, u32[]{:S(2)}, u32[]{:S(2)}) async-start(bf16[4,16,512]{2,1,0:T(8,128)(2,1)} %broadcast_select_fusion), calls=%async_computation.2 | async-start | bytes 131072 | tf_op jit(solution)/shard_map/all_to_all | solution.py:12
  53.1 65.5 %reduce-scatter.2.cloned.1.call-start = ((), (), s32[]{:S(2)}) async-start(), calls=%async_computation.5 | async-start | bytes 5898240 | tf_op jit(solution)/shard_map/reduce_scatter | solution.py:86
  58.9 1.7 copy-start.2
  63.5 99.2 %all-reduce.2.cloned.1.call-start = ((), (), s32[]{:S(2)}) async-start(), calls=%async_computation.6 | async-start | bytes 1310720 | tf_op jit(solution)/shard_map/psum | solution.py:87
  118.7 14.9 %copy-start.4 = (bf16[512,512]{1,0:T(8,128)(2,1)S(1)}, bf16[512,512]{1,0:T(8,128)(2,1)}, u32[]{:S(2)}) copy-start(bf16[512,512]{1,0:T(8,128)(2,1)} %param.12) | copy-start | bytes 1572868
Sparse Core Ops, SparseCore 0:
  63.6 54.9 reduce-scatter.1
  121.0 41.6 all-reduce.1
where the time goes:
time: 172 us; the launch traced here: 171 us
  waiting for transfers between devices  92.4 us (54%)
  other arithmetic  18.9 us (11%)
  starting transfers between devices  15.4 us (9%)
  between operations  14.2 us (8%)
  matrix products  11.9 us (7%)
  blocking collectives  11.1 us (6%)
  local copies, waits for them, and re-layouts  7.62 us (4%)
    reduce_scatter x1, waiting for transfers between devices, per_device(): lax.psum_scatter(local_grads, 'grp', scatter_dimension=1, tiled=True)  55.1 us
    psum x1, waiting for transfers between devices, per_device(): weight_grads = lax.psum(group_part, 'dom')  27.2 us
    scatter-add x1, other arithmetic, edge_counts(): jax.ops.segment_sum(ones, flat_index, num_segments=relations * local_rows...  11.4 us
    all_to_all x1, blocking collectives, push_rows(): lax.all_to_all(mirror_part.reshape(domains, -1, width), 'dom', split_axis...  11.1 us
    all_to_all x2, starting transfers between devices, pull_rows(): lax.all_to_all(picked.reshape(domains, -1, width), 'dom', split_axis=0, c...  10.2 us
    all_to_all x1, waiting for transfers between devices, push_rows(): lax.all_to_all(mirror_part.reshape(domains, -1, width), 'dom', split_axis...  5.66 us
    all_to_all x1, starting transfers between devices, push_rows(): lax.all_to_all(mirror_part.reshape(domains, -1, width), 'dom', split_axis...  5.08 us
    all_to_all x2, waiting for transfers between devices, pull_rows(): lax.all_to_all(picked.reshape(domains, -1, width), 'dom', split_axis=0, c...  4.44 us
  transfers between devices with their start and end apart: 5, of which 4 were waited for; matrix products, arithmetic and copies ran while one was open for 11% of the time, Pallas kernels for 0%

commit v1 on v0

--- a/solution.py
+++ b/solution.py
@@ -84,7 +84,13 @@
     self_grad = jnp.dot(masters.T, grad_z, preferred_element_type=jnp.float32)
     local_grads = jnp.concatenate([relation_grad, self_grad[None]], axis=0)
     group_part = lax.psum_scatter(local_grads, "grp", scatter_dimension=1, tiled=True)
-    weight_grads = lax.psum(group_part, "dom")
+    n_dev = lax.axis_size("dom")
+    weight_grads, far = (group_part, 1)
+    while far < n_dev:
+        weight_grads = weight_grads + lax.ppermute(
+            weight_grads, "dom", [(i, i ^ far) for i in range(n_dev)]
+        )
+        far = 2 * far
     back = jnp.einsum(
         "rij,id->rjd", adjacency, grad_table, preferred_element_type=jnp.float32
     ).astype(jnp.bfloat16)

time: 172 us -> 181 us (1.052)
  blocking collectives: 11.1 us -> 25.8 us
  waiting for transfers between devices: 92.4 us -> 80.3 us
  starting transfers between devices: 15.4 us -> 19.3 us
  other arithmetic: 18.9 us -> 22.1 us
    psum x1 -> x0, waiting for transfers between devices: 27.2 us -> none  [per_device(): weight_grads = lax.psum(group_part, 'dom')]
    ppermute x0 -> x2, waiting for transfers between devices: none -> 15 us  [per_device(): lax.ppermute(weight_grads, 'dom', [(i, i ^ far) for i in range(n_dev)])]
    all_to_all x1, blocking collectives: 11.1 us -> 25.8 us  [push_rows(): lax.all_to_all(mirror_part.reshape(domains, -1, width), 'dom', split_axis...]
    ppermute x0 -> x2, starting transfers between devices: none -> 3.97 us  [per_device(): lax.ppermute(weight_grads, 'dom', [(i, i ^ far) for i in range(n_dev)])]
    add x0 -> x2, other arithmetic: none -> 3.22 us  [per_device(): weight_grads + lax.ppermute(weight_grads, 'dom', [(i, i ^ far) for i in r...]
  transfers between devices with their start and end apart: 5 -> 6, of which waited for: 4 -> 4; matrix products, arithmetic and copies ran while one was open for 11% -> 11% of each run, Pallas kernels for 0% -> 0%
where the time goes in v1:
time: 181 us; the launch traced here: 180 us
  waiting for transfers between devices  80.3 us (44%)
  blocking collectives  25.8 us (14%)
  other arithmetic  22.1 us (12%)
  starting transfers between devices  19.3 us (11%)
  between operations  14.2 us (8%)
  matrix products  11.9 us (7%)
  local copies, waits for them, and re-layouts  6.25 us (3%)
    reduce_scatter x1, waiting for transfers between devices, per_device(): lax.psum_scatter(local_grads, 'grp', scatter_dimension=1, tiled=True)  55.1 us
    all_to_all x1, blocking collectives, push_rows(): lax.all_to_all(mirror_part.reshape(domains, -1, width), 'dom', split_axis...  25.8 us
    ppermute x2, waiting for transfers between devices, per_device(): lax.ppermute(weight_grads, 'dom', [(i, i ^ far) for i in range(n_dev)])  15 us
    scatter-add x1, other arithmetic, edge_counts(): jax.ops.segment_sum(ones, flat_index, num_segments=relations * local_rows...  11.4 us
    all_to_all x2, starting transfers between devices, pull_rows(): lax.all_to_all(picked.reshape(domains, -1, width), 'dom', split_axis=0, c...  10.2 us
    all_to_all x1, waiting for transfers between devices, push_rows(): lax.all_to_all(mirror_part.reshape(domains, -1, width), 'dom', split_axis...  5.66 us
    all_to_all x1, starting transfers between devices, push_rows(): lax.all_to_all(mirror_part.reshape(domains, -1, width), 'dom', split_axis...  5.09 us
    all_to_all x2, waiting for transfers between devices, pull_rows(): lax.all_to_all(picked.reshape(domains, -1, width), 'dom', split_axis=0, c...  4.44 us
  transfers between devices with their start and end apart: 6, of which 4 were waited for; matrix products, arithmetic and copies ran while one was open for 11% of the time, Pallas kernels for 0%

profile of v1, /device:TPU:0, one launch (start us, length us, event | category | flops | bytes accessed | tf_op | source)
XLA Modules:
  0.0 179.9 jit_solution(5536767361576202314)
XLA Ops:
  8.8 1.6 gather_fusion
  11.1 6.3 %all-to-all-start = ((bf16[4,16,512]{2,1,0:T(8,128)(2,1)}), bf16[4,16,512]{2,1,0:T(8,128)(2,1)S(1)}, u32[]{:S(2)}, u32[]{:S(2)}) async-start(bf16[4,16,512]{2,1,0:T(8,128)(2,1)} %broadcast_select_fusion.1), calls=%async_computation | async-start | bytes 131072 | tf_op jit(solution)/shard_map/all_to_all | solution.py:12
  18.2 11.4 %scatter_custom_fusion = f32[147456]{0:T(1024)S(1)} fusion(s32[2048]{0:T(1024)S(1)} %bitcast.65, f32[2048]{0:T(1024)S(1)} %broadcast.65, f32[]{:T(128)} %constant.6.clone.1), kind=kCustom, calls=%fused_computation.16 | custom fusion | flops 2048 | bytes 589828 | tf_op jit(solution)/shard_map/scatter-add | solution.py:30
  30.6 1.2 convolution_convert_fusion.1
  33.8 5.1 %all-to-all-start.1 = ((bf16[4,16,512]{2,1,0:T(8,128)(2,1)}), bf16[4,16,512]{2,1,0:T(8,128)(2,1)S(1)}, u32[]{:S(2)}, u32[]{:S(2)}) async-start(bf16[4,16,512]{2,1,0:T(8,128)(2,1)} %bitcast.10), calls=%async_computation.1 | async-start | bytes 131072 | tf_op jit(solution)/shard_map/all_to_all | solution.py:21
  38.9 5.7 %all-to-all-done.1 = bf16[4,16,512]{2,1,0:T(8,128)(2,1)S(1)} async-done(((bf16[4,16,512]{2,1,0:T(8,128)(2,1)}), bf16[4,16,512]{2,1,0:T(8,128)(2,1)S(1)}, u32[]{:S(2)}, u32[]{:S(2)}) %all-to-all-start.1) | async-done | bytes 65568 | tf_op jit(solution)/shard_map/all_to_all | solution.py:21
  44.8 2.2 %fusion.9 = (bf16[128,512]{1,0:T(8,128)(2,1)S(1)}, bf16[1,128,512]{2,1,0:T(8,128)(2,1)}) fusion(bf16[1,128,512]{2,1,0:T(8,128)(2,1)} %param.10, f32[128,512]{1,0:T(8,128)S(1)} %fusion.17, bf16[512,512]{1,0:T(8,128)(2,1)} %param.12, bf16[1,128,512]{2,1,0:T(8,128)(2,1)S(1)} %copy-done.1, f32[192,512]{1,0:T(8,128)} %copy-done.3), kind=kOutput, calls=%fused_computation.20 | convolution fusion | flops 68026368 | bytes 1572864 | tf_op jit(solution)/shard_map/dot_general | solution.py:71
  46.9 1.3 gather_fusion.1
  48.3 1.5 broadcast_select_fusion
  49.8 3.9 %all-to-all-start.2 = ((bf16[4,16,512]{2,1,0:T(8,128)(2,1)}), bf16[4,16,512]{2,1,0:T(8,128)(2,1)}, u32[]{:S(2)}, u32[]{:S(2)}) async-start(bf16[4,16,512]{2,1,0:T(8,128)(2,1)} %broadcast_select_fusion), calls=%async_computation.2 | async-start | bytes 131072 | tf_op jit(solution)/shard_map/all_to_all | solution.py:12
  53.8 1.3 convolution_bitcast_fusion
  55.1 4.4 %all-to-all-done.2 = bf16[4,16,512]{2,1,0:T(8,128)(2,1)} async-done(((bf16[4,16,512]{2,1,0:T(8,128)(2,1)}), bf16[4,16,512]{2,1,0:T(8,128)(2,1)}, u32[]{:S(2)}, u32[]{:S(2)}) %all-to-all-start.2) | async-done | bytes 65568 | tf_op jit(solution)/shard_map/all_to_all | solution.py:12
  59.5 1.7 fusion.13
  61.2 2.9 %pad_maximum_fusion = f32[5,512,512]{2,1,0:T(8,128)} fusion(f32[1,512,512]{2,1,0:T(8,128)S(1)} %copy-done.2, f32[4,512,512]{2,1,0:T(8,128)S(1)} %fusion.13), kind=kLoop, calls=%fused_computation.3 | loop fusion | flops 1310720 | bytes 10485760 | tf_op jit(solution)/shard_map/concatenate | solution.py:85
  64.1 55.1 %reduce-scatter.2.cloned.1.call-done = f32[5,64,512]{2,1,0:T(8,128)} async-done(((f32[5,512,512]{2,1,0:T(8,128)}), f32[5,64,512]{2,1,0:T(8,128)}) %reduce-scatter.2.cloned.1.call-update) | async-done | bytes 655376 | tf_op jit(solution)/shard_map/reduce_scatter | solution.py:86
  119.2 1.5 collective-permute-start
  120.7 15.0 %collective-permute-done = f32[5,64,512]{2,1,0:T(8,128)S(1)} collective-permute-done((f32[5,64,512]{2,1,0:T(8,128)}, f32[5,64,512]{2,1,0:T(8,128)S(1)}, u32[]{:S(2)}, u32[]{:S(2)}) %collective-permute-start) | collective-permute-done | bytes 655392 | tf_op jit(solution)/shard_map/ppermute | solution.py:90
  135.8 1.2 add.75
  137.0 2.5 %collective-permute-start.1 = (f32[5,64,512]{2,1,0:T(8,128)S(1)}, f32[5,64,512]{2,1,0:T(8,128)}, u32[]{:S(2)}, u32[]{:S(2)}) collective-permute-start(f32[5,64,512]{2,1,0:T(8,128)S(1)} %add.75), channel_id=1, source_target_pairs={{0,16},{8,24},{16,0},{24,8},{1,17},{9,25},{17,1},{25,9},{2,18},{10... | collective-permute-start | bytes 1966088 | tf_op jit(solution)/shard_map/ppermute | solution.py:90
  139.4 2.6 %fusion.1 = f32[192,512]{1,0:T(8,128)} fusion(bf16[4,512,512]{2,1,0:T(8,128)(2,1)S(1)} %copy-done, bf16[4,192,192]{2,1,0:T(8,128)(2,1)S(1)} %convert_element_type.31, bf16[64,512]{1,0:T(8,128)(2,1)} %bitcast.15, bf16[128,512]{1,0:T(8,128)(2,1)S(1)} %get-tuple-element.3), kind=kOutput, calls=%fused_computation.8 | convolution fusion | flops 554434560 | bytes 2981888 | tf_op jit(solution)/shard_map/rne,rde->nd/dot_general | solution.py:97
  142.1 0.9 slice.30
  143.0 25.8 %all_to_all.20 = bf16[4,16,512]{2,1,0:T(8,128)(2,1)S(1)} all-to-all(bf16[4,16,512]{2,1,0:T(8,128)(2,1)S(1)} %bitcast.61), channel_id=1, replica_groups=mesh['dom'=4,'grp'=8] {'dom'}, dimensions={0} | all-to-all | bytes 131072 | tf_op jit(solution)/shard_map/all_to_all | solution.py:21
  169.0 2.1 %fusion.5 = bf16[1,128,512]{2,1,0:T(8,128)(2,1)} fusion(f32[128,512]{1,0:T(8,128)S(1)} %fusion.15, bf16[128,512]{1,0:T(8,128)(2,1)S(1)} %get-tuple-element.3, bf16[512,512]{1,0:T(8,128)(2,1)} %param.12, f32[192,512]{1,0:T(8,128)} %fusion.1), kind=kOutput, calls=%fused_computation.15 | convolution fusion | flops 67305472 | bytes 1310720 | tf_op jit(solution)/shard_map/dot_general | solution.py:100
  171.1 2.0 %add.76 = f32[5,64,512]{2,1,0:T(8,128)} add(f32[5,64,512]{2,1,0:T(8,128)S(1)} %add.75, f32[5,64,512]{2,1,0:T(8,128)} %collective-permute-done.1) | non-fusion elementwise | flops 163840 | bytes 1966080 | tf_op jit(solution)/shard_map/add | solution.py:90
  (29 shorter events, 6.4 us)
Async XLA Ops:
  7.2 24.6 %copy-start = (bf16[4,512,512]{2,1,0:T(8,128)(2,1)S(1)}, bf16[4,512,512]{2,1,0:T(8,128)(2,1)}, u32[]{:S(2)}) copy-start(bf16[4,512,512]{2,1,0:T(8,128)(2,1)} %param.11) | copy-start | bytes 6291460
  7.2 23.4 %copy-start.1 = (bf16[1,128,512]{2,1,0:T(8,128)(2,1)S(1)}, bf16[1,128,512]{2,1,0:T(8,128)(2,1)}, u32[]{:S(2)}) copy-start(bf16[1,128,512]{2,1,0:T(8,128)(2,1)} %param.9) | copy-start | bytes 393220
  11.1 18.8 %all-to-all-start = ((bf16[4,16,512]{2,1,0:T(8,128)(2,1)}), bf16[4,16,512]{2,1,0:T(8,128)(2,1)S(1)}, u32[]{:S(2)}, u32[]{:S(2)}) async-start(bf16[4,16,512]{2,1,0:T(8,128)(2,1)} %broadcast_select_fusion.1), calls=%async_computation | async-start | bytes 131072 | tf_op jit(solution)/shard_map/all_to_all | solution.py:12
  29.9 0.6 copy-start.4
  31.8 12.8 %copy-start.5 = (s32[1,64]{1,0:T(1,128)S(1)}, s32[1,64]{1,0:T(1,128)}, u32[]{:S(2)}) copy-start(s32[1,64]{1,0:T(1,128)} %param.16) | copy-start | bytes 772
  32.4 0.7 copy-start.3
  33.8 10.8 %all-to-all-start.1 = ((bf16[4,16,512]{2,1,0:T(8,128)(2,1)}), bf16[4,16,512]{2,1,0:T(8,128)(2,1)S(1)}, u32[]{:S(2)}, u32[]{:S(2)}) async-start(bf16[4,16,512]{2,1,0:T(8,128)(2,1)} %bitcast.10), calls=%async_computation.1 | async-start | bytes 131072 | tf_op jit(solution)/shard_map/all_to_all | solution.py:21
  49.8 9.7 %all-to-all-start.2 = ((bf16[4,16,512]{2,1,0:T(8,128)(2,1)}), bf16[4,16,512]{2,1,0:T(8,128)(2,1)}, u32[]{:S(2)}, u32[]{:S(2)}) async-start(bf16[4,16,512]{2,1,0:T(8,128)(2,1)} %broadcast_select_fusion), calls=%async_computation.2 | async-start | bytes 131072 | tf_op jit(solution)/shard_map/all_to_all | solution.py:12
  53.7 65.5 %reduce-scatter.2.cloned.1.call-start = ((), (), s32[]{:S(2)}) async-start(), calls=%async_computation.5 | async-start | bytes 5898240 | tf_op jit(solution)/shard_map/reduce_scatter | solution.py:86
  59.5 1.7 copy-start.2
  119.2 16.5 %collective-permute-start = (f32[5,64,512]{2,1,0:T(8,128)}, f32[5,64,512]{2,1,0:T(8,128)S(1)}, u32[]{:S(2)}, u32[]{:S(2)}) collective-permute-start(f32[5,64,512]{2,1,0:T(8,128)} %reduce-scatter.2.cloned.1.call-done), channel_id=1, source_target_pairs={{0,8},{8,0},{16,24},{24,16},{1,9},{9,1},{17,25},{25,17},{2,10},{10... | collective-permute-start | bytes 1966088 | tf_op jit(solution)/shard_map/ppermute | solution.py:90
  137.0 34.1 %collective-permute-start.1 = (f32[5,64,512]{2,1,0:T(8,128)S(1)}, f32[5,64,512]{2,1,0:T(8,128)}, u32[]{:S(2)}, u32[]{:S(2)}) collective-permute-start(f32[5,64,512]{2,1,0:T(8,128)S(1)} %add.75), channel_id=1, source_target_pairs={{0,16},{8,24},{16,0},{24,8},{1,17},{9,25},{17,1},{25,9},{2,18},{10... | collective-permute-start | bytes 1966088 | tf_op jit(solution)/shard_map/ppermute | solution.py:90
Sparse Core Ops, SparseCore 0:
  64.2 54.9 reduce-scatter.1
